TPU v7x, 32 devices: a whole 2x2x4 slice. The times are simulated.
32 devices in a mesh: gx: 2 (over core), gy: 4 (over y, x), gz: 4 (over z).
Axes of the slice: x: 2, y: 2, z: 4, core: 2. Of those that a mesh axis runs over, the one named last changes fastest.
Arguments:
- quant_codes: int32 [64, 128, 512], P('gx', 'gy', 'gz'), may hold values from -1073741824 to 1073741824, as said below
- error_step: float32 [1], replicated, may hold values from 4e-09 to 1.5e-08
Outputs:
- decoded: float32 [64, 128, 512], P('gx', 'gy', 'gz')
Inputs may be any that keep to these rules, and one draw needn't show every extreme that they name: quant_codes are the third differences (along the three dimensions, with zeros before the grid's first cells) of a field of integers between -134217728 and 134217728.
All inputs are finite; a program needn't handle non-finite values.
Results may differ from a plain program's by a relative error of at most 0.00002.
Values sent between devices are 32-bit elements; how exact they have to be, the bound alone decides.
A program may use at most 64 MiB of HBM per device.

v0:
```python
import jax
import jax.numpy as jnp
from jax import lax
from jax.sharding import PartitionSpec as P


def prefix_2(value, axis, combine, identity):
    size, position = (lax.axis_size(axis), lax.axis_index(axis))
    everything = lax.all_gather(value, axis)
    start = jnp.broadcast_to(jnp.asarray(identity, value.dtype), value.shape)

    def turn(k, before):
        reached = k < position
        new = combine(before, everything[k])
        return jnp.where(reached, new, before)

    return lax.fori_loop(0, size, turn, start)


def passed_along(block, axis, distance):
    devices = range(lax.axis_size(axis))
    route = [(i - distance, i) for i in devices if i - distance in devices]
    return lax.ppermute(block, axis, route)


def add_terms(earlier, later):
    return jax.tree.map(jnp.add, earlier, later)


def cumulate(values, axis_dim):
    length = values.shape[axis_dim]
    position = lax.broadcasted_iota(jnp.int32, values.shape, axis_dim)
    offset = 1
    while offset < length:
        rolled = jnp.roll(values, offset, axis_dim)
        values = values + jnp.where(position >= offset, rolled, jnp.zeros_like(rolled))
        offset = offset * 2
    return values


def beside(values, low_plane, high_plane, axis_dim):
    length = values.shape[axis_dim]
    position = lax.broadcasted_iota(jnp.int32, values.shape, axis_dim)
    below = jnp.where(
        position == 0, jnp.expand_dims(low_plane, axis_dim), jnp.roll(values, 1, axis_dim)
    )
    above = jnp.where(
        position == length - 1,
        jnp.expand_dims(high_plane, axis_dim),
        jnp.roll(values, -1, axis_dim),
    )
    return below + above


def on_device(quant_codes, error_step):
    step_size = error_step[0]
    sectioned = cumulate(quant_codes, 0)
    x_face = sectioned[-1]
    carry_x = prefix_2(x_face, "gx", add_terms, jnp.zeros_like(x_face))
    sectioned = cumulate(sectioned + carry_x[None], 1)
    y_face = sectioned[:, -1, :]
    carry_y = prefix_2(y_face, "gy", add_terms, jnp.zeros_like(y_face))
    sectioned = cumulate(sectioned + carry_y[:, None, :], 2)
    z_face = sectioned[:, :, -1]
    carry_z = prefix_2(z_face, "gz", add_terms, jnp.zeros_like(z_face))
    prefix = sectioned + carry_z[:, :, None]
    recon = prefix.astype(jnp.float32) * step_size
    below_x = passed_along(recon[-1], "gx", 1)
    below_y = passed_along(recon[:, -1, :], "gy", 1)
    below_z = passed_along(recon[:, :, -1], "gz", 1)
    above_x = passed_along(recon[0], "gx", -1)
    above_y = passed_along(recon[:, 0, :], "gy", -1)
    above_z = passed_along(recon[:, :, 0], "gz", -1)
    neighbours = beside(recon, below_x, above_x, 0)
    neighbours = neighbours + beside(recon, below_y, above_y, 1)
    neighbours = neighbours + beside(recon, below_z, above_z, 2)
    return recon + 0.5 * (neighbours / 6.0 - recon)


def solution(mesh):
    in_specs = (P("gx", "gy", "gz"), P())
    out_specs = P("gx", "gy", "gz")
    return jax.shard_map(
        on_device, mesh=mesh, in_specs=in_specs, out_specs=out_specs, check_vma=False
    )
```

profile of v0, /device:TPU:0, one launch (start us, length us, event | category | flops | bytes accessed | tf_op | source)
XLA Modules:
  0.0 81.4 jit_solution(14851864983315675783)
XLA Ops:
  0.0 1.1 %slice.248 = s32[31,32,128]{2,1,0:T(8,128)S(1)} slice(s32[32,32,128]{2,1,0:T(8,128)} %param.8), slice={[0:31], [0:32], [0:128]} | slice | bytes 1015808 | tf_op jit(solution)/shard_map/jit(_roll_static)/slice | solution.py:35
  1.2 0.3 copy.37
  1.5 0.4 fusion
  1.9 0.1 fusion.1
  2.1 0.1 fusion.2
  2.3 0.1 fusion.3
  2.5 0.1 fusion.4
  2.7 2.0 %all_gather.9 = s32[2,32,128]{2,1,0:T(8,128)S(1)} all-gather(s32[1,32,128]{2,1,0:T(8,128)S(1)} %bitcast.48), channel_id=1, replica_groups=mesh['gx'=2,'gy'=4,'gz'=4] {'gx'}, dimensions={0}, use_global_device_ids=true | all-gather | bytes 49152 | tf_op jit(solution)/shard_map/all_gather | solution.py:9
  4.8 0.1 fusion.5
  5.0 0.1 fusion.6
  5.2 0.1 fusion.7
  5.5 0.1 fusion.8
  5.6 0.1 fusion.9
  5.8 9.6 %all-gather = s32[128,1,128]{2,0,1:T(8,128)S(1)} all-gather(s32[32,1,128]{2,0,1:T(8,128)S(1)} %slice.268), channel_id=2, replica_groups=mesh['gx'=2,'gy'=4,'gz'=4] {'gy'}, dimensions={0}, use_global_device_ids=true | all-gather | bytes 81920 | tf_op jit(solution)/shard_map/all_gather | solution.py:9
  15.4 0.1 while.43
  15.6 0.2 slice.269
  15.8 0.2 fusion.10
  16.0 0.2 slice.271
  16.2 0.2 fusion.11
  16.4 0.2 slice.273
  16.6 0.2 fusion.12
  16.8 0.2 slice.275
  17.0 0.2 fusion.13
  17.3 0.2 slice.277
  17.5 0.2 fusion.14
  17.7 0.2 slice.279
  17.9 0.2 fusion.15
  18.1 0.2 fusion.31
  19.0 0.2 fusion.16
  19.2 0.2 slice.283
  19.4 36.9 %all-gather.1 = s32[128,32,1]{2,0,1:T(8,128)S(1)} all-gather(s32[32,32,1]{2,0,1:T(8,128)S(1)} %slice.283), channel_id=3, replica_groups=mesh['gx'=2,'gy'=4,'gz'=4] {'gz'}, dimensions={0}, use_global_device_ids=true | all-gather | bytes 20480 | tf_op jit(solution)/shard_map/all_gather | solution.py:9
  56.3 1.1 %copy.35 = s32[128,32,1]{1,0,2:T(8,128)S(1)} copy(s32[128,32,1]{2,0,1:T(8,128)S(1)} %all-gather.1) | data formatting | bytes 32768
  57.4 0.1 while.44
  57.6 0.2 convert_multiply_fusion
  57.8 0.2 fusion.27
  58.1 0.4 copy.32
  58.4 1.3 %collective-permute-start.5 = (f32[32,32]{1,0:T(8,128)S(1)}, f32[32,32]{1,0:T(8,128)S(1)}, u32[]{:S(2)}, u32[]{:S(2)}) collective-permute-start(f32[32,32]{1,0:T(8,128)S(1)} %bitcast.50), channel_id=1, source_target_pairs={{1,0},{2,1},{3,2},{5,4},{6,5},{7,6},{9,8},{10,9},{11,10},{13,12},{... | collective-permute-start | bytes 12296 | tf_op jit(solution)/shard_map/ppermute | solution.py:23
  59.7 0.4 copy.30
  60.1 4.5 %collective-permute-start.4 = (f32[32,32]{1,0:T(8,128)S(1)}, f32[32,32]{1,0:T(8,128)S(1)}, u32[]{:S(2)}, u32[]{:S(2)}) collective-permute-start(f32[32,32]{1,0:T(8,128)S(1)} %bitcast.49), channel_id=1, source_target_pairs={{0,1},{1,2},{2,3},{4,5},{5,6},{6,7},{8,9},{9,10},{10,11},{12,13},{... | collective-permute-start | bytes 12296 | tf_op jit(solution)/shard_map/ppermute | solution.py:23
  64.6 1.3 %collective-permute-start.3 = (f32[32,128]{1,0:T(8,128)S(1)}, f32[32,128]{1,0:T(8,128)S(1)}, u32[]{:S(2)}, u32[]{:S(2)}) collective-permute-start(f32[32,128]{1,0:T(8,128)S(1)} %get-tuple-element.339), channel_id=1, source_target_pairs={{4,0},{8,4},{12,8},{5,1},{9,5},{13,9},{6,2},{10,6},{14,10},{7,3},{... | collective-permute-start | bytes 49160 | tf_op jit(solution)/shard_map/ppermute | solution.py:23
  65.9 4.5 %collective-permute-start.2 = (f32[32,128]{1,0:T(8,128)S(1)}, f32[32,128]{1,0:T(8,128)S(1)}, u32[]{:S(2)}, u32[]{:S(2)}) collective-permute-start(f32[32,128]{1,0:T(8,128)S(1)} %get-tuple-element.338), channel_id=1, source_target_pairs={{0,4},{4,8},{8,12},{1,5},{5,9},{9,13},{2,6},{6,10},{10,14},{3,7},{... | collective-permute-start | bytes 49160 | tf_op jit(solution)/shard_map/ppermute | solution.py:23
  70.5 1.3 %collective-permute-start.1 = (f32[32,128]{1,0:T(8,128)S(1)}, f32[32,128]{1,0:T(8,128)S(1)}, u32[]{:S(2)}, u32[]{:S(2)}) collective-permute-start(f32[32,128]{1,0:T(8,128)S(1)} %bitcast.46), channel_id=1, source_target_pairs={{16,0},{17,1},{18,2},{19,3},{20,4},{21,5},{22,6},{23,7},{24,8},{25... | collective-permute-start | bytes 49160 | tf_op jit(solution)/shard_map/ppermute | solution.py:23
  71.9 1.1 %fusion.28 = (f32[32,31,128]{2,0,1:T(8,128)}, f32[32,31,128]{2,0,1:T(8,128)}) fusion(f32[32,32,128]{2,0,1:T(8,128)S(1)} %convert_multiply_fusion), kind=kLoop, calls=%fused_computation.75 | loop fusion | bytes 2031616 | tf_op jit(solution)/shard_map/jit(_roll_static)/slice | solution.py:50
  73.0 1.1 %fusion.26 = (f32[32,32,127]{2,0,1:T(8,128)}, f32[32,32,127]{2,0,1:T(8,128)}) fusion(f32[32,32,128]{2,0,1:T(8,128)S(1)} %convert_multiply_fusion), kind=kLoop, calls=%fused_computation.73 | loop fusion | bytes 2080768 | tf_op jit(solution)/shard_map/jit(_roll_static)/slice | solution.py:50
  74.2 3.0 %collective-permute-start = (f32[32,128]{1,0:T(8,128)S(1)}, f32[32,128]{1,0:T(8,128)S(1)}, u32[]{:S(2)}, u32[]{:S(2)}) collective-permute-start(f32[32,128]{1,0:T(8,128)S(1)} %bitcast.47), channel_id=1, source_target_pairs={{0,16},{1,17},{2,18},{3,19},{4,20},{5,21},{6,22},{7,23},{8,24},{9,... | collective-permute-start | bytes 49160 | tf_op jit(solution)/shard_map/ppermute | solution.py:23
  77.4 0.6 collective-permute-done
  78.0 2.3 %fusion.23 = f32[32,32,128]{2,0,1:T(8,128)S(1)} fusion(f32[31,32,128]{2,0,1:T(8,128)S(1)} %get-tuple-element.349, f32[1,32,128]{2,0,1:T(1,128)S(1)} %get-tuple-element.351, f32[1,32,128]{2,0,1:T(1,128)S(1)} %get-tuple-element.350, f32[31,32,128]{2,0,1:T(8,128)S(1)} %get-tuple-element.348, f32[32,31,128]{2,0,1:T(8,128)} %get-tuple-element.347, ...), kind=kLoop, calls=%fused_computation.44 | loop fusion | flops 3145728 | bytes 4272452 | tf_op jit(solution)/shard_map/add | solution.py:77
  80.3 1.1 %copy.34 = f32[32,32,128]{2,1,0:T(8,128)} copy(f32[32,32,128]{2,0,1:T(8,128)S(1)} %fusion.23) | data formatting | bytes 1048576 | tf_op jit(solution)/shard_map/add | solution.py:77
  (61 shorter events, 1.0 us)
Async XLA Ops:
  0.0 1.5 %copy-start = (s32[32,32,128]{2,1,0:T(8,128)S(1)}, s32[32,32,128]{2,1,0:T(8,128)}, u32[]{:S(2)}) copy-start(s32[32,32,128]{2,1,0:T(8,128)} %param.8) | copy-start | bytes 1572868
  0.0 1.5 %slice-start = ((s32[32,32,128]{2,1,0:T(8,128)}), s32[1,32,128]{2,1,0:T(8,128)S(1)}, s32[]{:S(2)}) async-start(s32[32,32,128]{2,1,0:T(8,128)} %param.8), calls=%async_computation | async-start | bytes 32768 | tf_op jit(solution)/shard_map/jit(_roll_static)/slice | solution.py:35
  58.4 15.8 %collective-permute-start.5 = (f32[32,32]{1,0:T(8,128)S(1)}, f32[32,32]{1,0:T(8,128)S(1)}, u32[]{:S(2)}, u32[]{:S(2)}) collective-permute-start(f32[32,32]{1,0:T(8,128)S(1)} %bitcast.50), channel_id=1, source_target_pairs={{1,0},{2,1},{3,2},{5,4},{6,5},{7,6},{9,8},{10,9},{11,10},{13,12},{... | collective-permute-start | bytes 12296 | tf_op jit(solution)/shard_map/ppermute | solution.py:23
  60.1 17.2 %collective-permute-start.4 = (f32[32,32]{1,0:T(8,128)S(1)}, f32[32,32]{1,0:T(8,128)S(1)}, u32[]{:S(2)}, u32[]{:S(2)}) collective-permute-start(f32[32,32]{1,0:T(8,128)S(1)} %bitcast.49), channel_id=1, source_target_pairs={{0,1},{1,2},{2,3},{4,5},{5,6},{6,7},{8,9},{9,10},{10,11},{12,13},{... | collective-permute-start | bytes 12296 | tf_op jit(solution)/shard_map/ppermute | solution.py:23
  64.6 12.8 %collective-permute-start.3 = (f32[32,128]{1,0:T(8,128)S(1)}, f32[32,128]{1,0:T(8,128)S(1)}, u32[]{:S(2)}, u32[]{:S(2)}) collective-permute-start(f32[32,128]{1,0:T(8,128)S(1)} %get-tuple-element.339), channel_id=1, source_target_pairs={{4,0},{8,4},{12,8},{5,1},{9,5},{13,9},{6,2},{10,6},{14,10},{7,3},{... | collective-permute-start | bytes 49160 | tf_op jit(solution)/shard_map/ppermute | solution.py:23
  65.9 11.5 %collective-permute-start.2 = (f32[32,128]{1,0:T(8,128)S(1)}, f32[32,128]{1,0:T(8,128)S(1)}, u32[]{:S(2)}, u32[]{:S(2)}) collective-permute-start(f32[32,128]{1,0:T(8,128)S(1)} %get-tuple-element.338), channel_id=1, source_target_pairs={{0,4},{4,8},{8,12},{1,5},{5,9},{9,13},{2,6},{6,10},{10,14},{3,7},{... | collective-permute-start | bytes 49160 | tf_op jit(solution)/shard_map/ppermute | solution.py:23
  70.5 6.9 %collective-permute-start.1 = (f32[32,128]{1,0:T(8,128)S(1)}, f32[32,128]{1,0:T(8,128)S(1)}, u32[]{:S(2)}, u32[]{:S(2)}) collective-permute-start(f32[32,128]{1,0:T(8,128)S(1)} %bitcast.46), channel_id=1, source_target_pairs={{16,0},{17,1},{18,2},{19,3},{20,4},{21,5},{22,6},{23,7},{24,8},{25... | collective-permute-start | bytes 49160 | tf_op jit(solution)/shard_map/ppermute | solution.py:23
  74.2 3.9 %collective-permute-start = (f32[32,128]{1,0:T(8,128)S(1)}, f32[32,128]{1,0:T(8,128)S(1)}, u32[]{:S(2)}, u32[]{:S(2)}) collective-permute-start(f32[32,128]{1,0:T(8,128)S(1)} %bitcast.47), channel_id=1, source_target_pairs={{0,16},{1,17},{2,18},{3,19},{4,20},{5,21},{6,22},{7,23},{8,24},{9,... | collective-permute-start | bytes 49160 | tf_op jit(solution)/shard_map/ppermute | solution.py:23
where the time goes:
time: 81.7 us; the launch traced here: 81.4 us
  blocking collectives  48.5 us (59%)
  starting transfers between devices  16 us (20%)
  local copies, waits for them, and re-layouts  9.16 us (11%)
  other arithmetic  5.75 us (7%)
  between operations  1.21 us (1%)
    all_gather x3, blocking collectives, prefix_2(): everything = lax.all_gather(value, axis)  48.5 us
    ppermute x6, starting transfers between devices, passed_along(): return lax.ppermute(block, axis, route)  16 us
    add x17, other arithmetic, cumulate(): values + jnp.where(position >= offset, rolled, jnp.zeros_like(rolled))  2.98 us
    slice x24, local copies, waits for them, and re-layouts, cumulate(): rolled = jnp.roll(values, offset, axis_dim)  2.87 us
    slice x3, local copies, waits for them, and re-layouts, beside(): jnp.roll(values, -1, axis_dim)  2.35 us
    add x1, other arithmetic, on_device(): return recon + 0.5 * (neighbours / 6.0 - recon)  2.3 us
  transfers between devices with their start and end apart: 6, of which 1 were waited for; matrix products, arithmetic and copies ran while one was open for 4% of the time, Pallas kernels for 0%

commit v1 on v0

v1 whole, which is shorter than its diff:
```python
import functools

import jax
import jax.numpy as jnp
from jax import lax
from jax.experimental import pallas as pl
from jax.experimental.pallas import tpu as pltpu
from jax.sharding import PartitionSpec as P

MESH = pl.DeviceIdType.MESH
I32 = jnp.int32
F32 = jnp.float32
SUB = 8


def iota(shape, dim):
    return lax.broadcasted_iota(I32, shape, dim)


def turn(x, by, dim):
    n = x.shape[dim]
    by = by % n
    if by == 0:
        return x
    if dim == 1 and n % 128 != 0:
        return jnp.concatenate([x[:, n - by :], x[:, : n - by]], 1)
    return pltpu.roll(x, by, dim)


def lane_scan(x):
    n = x.shape[1]
    tri = (iota((n, n), 0) <= iota((n, n), 1)).astype(F32)
    one, big = tri.astype(jnp.bfloat16), (tri * 256.0).astype(jnp.bfloat16)

    def times(part, m):
        return jnp.dot(part.astype(F32).astype(jnp.bfloat16), m, preferred_element_type=F32)

    low = times(x & 255, one) + times((x >> 8) & 255, big)
    high = times((x >> 16) & 255, one) + times(x >> 24, big)
    return low.astype(I32) + (high.astype(I32) << 16)


def row_scan(x):
    rows, n = x.shape
    s = iota((SUB, n), 0)
    out, carry = [], None
    for b in range(rows // SUB):
        v = x[b * SUB : (b + 1) * SUB]
        for d in (1, 2, 4):
            v = v + jnp.where(s >= d, pltpu.roll(v, d, 0), 0)
        if carry is not None:
            v = v + carry
        carry = jnp.broadcast_to(v[SUB - 1 : SUB], (SUB, n))
        out.append(v)
    return jnp.concatenate(out, 0) if len(out) > 1 else out[0]


def exchange(
    mesh_sizes, q_hbm, v_ref, eh_ref,
    q, scan, xs, xup, xdn, ys, yt, yup, ytup, hy, ht, ydn, ytdn,
    z0, z2, z1, zup0, zup2, zup1, d0, d2, d1, zdn0, zdn2, zdn1,
    rx, hx, ry, ryt, ax, hxc, by, hyc, za0, za2, za1,
    load_sem, xss, xrs, yss, yrs, ytss, ytrs, z0ss, z0rs, z2ss, z2rs, z1ss, z1rs, dss, drs,
):
    nx, ny, nz = mesh_sizes
    ni, nj, nk = q.shape
    nb = nj // SUB
    nl = ni * nb
    X, Y, Z = (lax.axis_index(a) for a in ("gx", "gy", "gz"))
    place = {"gx": X, "gy": Y, "gz": Z}
    size = {"gx": nx, "gy": ny, "gz": nz}
    last_x, last_y, last_z = X == nx - 1, Y == ny - 1, Z == nz - 1

    load = pltpu.make_async_copy(q_hbm, q, load_sem)
    load.start()
    barrier = pltpu.get_barrier_semaphore()
    for axis in ("gz", "gy", "gx"):
        for d in range(1, size[axis]):
            pl.semaphore_signal(
                barrier, inc=1, device_id={axis: lax.rem(place[axis] + d, size[axis])},
                device_id_type=MESH,
            )

    ends = []

    def up(axis, src, slots, ssem, rsem):
        for d in range(1, size[axis]):
            def copy(d=d):
                return pltpu.make_async_remote_copy(
                    src_ref=src, dst_ref=slots.at[d - 1], send_sem=ssem.at[d - 1],
                    recv_sem=rsem.at[d - 1], device_id={axis: place[axis] + d},
                    device_id_type=MESH,
                )

            here = place[axis] + d < size[axis]

            @pl.when(here)
            def _():
                copy().start()

            ends.append((here, copy))

    def up_sum(axis, src, slots, ssem, rsem, total):
        total[...] = jnp.zeros_like(total)
        for d in range(1, size[axis]):
            @pl.when(place[axis] >= d)
            def _():
                pltpu.make_async_remote_copy(
                    src_ref=src, dst_ref=slots.at[d - 1], send_sem=ssem.at[d - 1],
                    recv_sem=rsem.at[d - 1], device_id={axis: place[axis]},
                    device_id_type=MESH,
                ).wait_recv()
                total[...] += slots[d - 1]

    def down_copy(axis, src, dst, n):
        return pltpu.make_async_remote_copy(
            src_ref=src, dst_ref=dst, send_sem=dss.at[n], recv_sem=drs.at[n],
            device_id={axis: place[axis] - 1}, device_id_type=MESH,
        )

    def down(axis, src, dst, n):
        here = place[axis] > 0

        @pl.when(here)
        def _():
            down_copy(axis, src, dst, n).start()

        ends.append((here, lambda: down_copy(axis, src, dst, n)))

    def down_wait(axis, src, dst, n):
        @pl.when(place[axis] < size[axis] - 1)
        def _():
            down_copy(axis, src, dst, n).wait_recv()

        @pl.when(place[axis] == size[axis] - 1)
        def _():
            dst[...] = jnp.zeros_like(dst)

    lanes = iota((SUB, nl), 1)
    subs = iota((SUB, nl), 0)

    load.wait()
    total = q[0]
    for i in range(1, ni):
        total = total + q[i]
    xs[...] = total
    pl.semaphore_wait(barrier, nx + ny + nz - 3)
    up("gx", xs, xup, xss, xrs)
    down("gx", q.at[0], xdn, 0)

    for i in range(ni):
        ys[pl.ds(i, 1), :] = jnp.sum(q[i], axis=0, keepdims=True)
        hy[pl.ds(i, 1), :] = q[i, 0:1, :]
    up("gy", ys, yup, yss, yrs)
    down("gy", hy, ydn, 1)

    step = 8

    def scan_block(g, _):
        rows = pl.ds(g * step, step)
        part = q[rows].reshape(step * nj, nk)
        scan[rows] = lane_scan(part).reshape(step, nj, nk)
        return 0

    lax.fori_loop(0, ni // step, scan_block, 0)

    up_sum("gx", xs, xup, xss, xrs, rx)
    down_wait("gx", q.at[0], xdn, 0)
    rxv, hxv = rx[...], xdn[...]
    sk = iota((SUB, nk), 0)
    yt[...] = jnp.where(
        sk == 0, jnp.sum(rxv, axis=0, keepdims=True),
        jnp.where(sk == 1, jnp.sum(hxv, axis=0, keepdims=True), 0),
    )
    ht[...] = jnp.where(sk == 0, rxv[0:1], 0)
    up("gy", yt, ytup, ytss, ytrs)
    down("gy", ht, ytdn, 2)

    a0 = jnp.zeros((SUB, nl), I32)
    b0 = jnp.zeros((SUB, nl), I32)
    for i in range(ni):
        for b in range(nb):
            rows = slice(b * SUB, (b + 1) * SUB)
            here = lanes == i * nb + b
            a0 = jnp.where(here, scan[i, rows, nk - 1 : nk], a0)
            b0 = jnp.where(here, q[i, rows, 0:1], b0)
    z0[...] = a0
    d0[...] = b0
    up("gz", z0, zup0, z0ss, z0rs)
    down("gz", d0, zdn0, 3)
    lx = lane_scan(jnp.concatenate([rxv, hxv], 0))
    a2 = jnp.zeros((SUB, nl), I32)
    b2 = jnp.zeros((SUB, nl), I32)
    for b in range(2 * nb):
        rows = slice(b * SUB, (b + 1) * SUB)
        a2 = jnp.where(lanes == b, lx[rows, nk - 1 : nk], a2)
        if b < nb:
            b2 = jnp.where(lanes == b, rxv[rows, 0:1], b2)
    z2[...] = a2
    d2[...] = b2
    up("gz", z2, zup2, z2ss, z2rs)
    down("gz", d2, zdn2, 4)
    ax[...] = row_scan(lx[:nj])
    hxc[...] = row_scan(lx[nj:])

    def cumulate(i, before):
        new = before + row_scan(scan[i])
        scan[i] = new
        return new

    lax.fori_loop(0, ni, cumulate, jnp.zeros((nj, nk), I32))

    up_sum("gy", ys, yup, yss, yrs, ry)
    up_sum("gy", yt, ytup, ytss, ytrs, ryt)
    down_wait("gy", hy, ydn, 1)
    down_wait("gy", ht, ytdn, 2)
    ryv, rytv = ry[...], ryt[...]
    ly = lane_scan(jnp.concatenate([ryv, ydn[...], rytv, ytdn[...]], 0))
    lyl, lyh = ly[:ni], ly[ni : 2 * ni]
    lyt, lyht = ly[2 * ni : 2 * ni + SUB], ly[2 * ni + SUB :]
    mine = (iota((ni, nl), 1) // nb) == iota((ni, nl), 0)
    first = (iota((1, nl), 1) // nb) == 0

    def along(column, extra):
        row = jnp.sum(jnp.where(mine, column, 0), axis=0, keepdims=True)
        return row + jnp.where(first, extra, 0)

    end = slice(nk - 1, nk)
    z1[...] = jnp.where(
        subs == 0, along(lyl[:, end], lyt[0:1, end]),
        jnp.where(
            subs == 1, along(lyh[:, end], lyht[0:1, end]),
            jnp.where(
                subs == 2, lyt[0:1, end], jnp.where(subs == 3, lyt[1:2, end], 0)
            ),
        ),
    )
    d1[...] = jnp.where(subs == 0, along(ryv[:, 0:1], rytv[0:1, 0:1]), 0)
    up("gz", z1, zup1, z1ss, z1rs)
    down("gz", d1, zdn1, 5)

    rows_i = iota((ni, nk), 0)
    by[...] = row_scan(lyl + jnp.where(rows_i == 0, lyt[0:1], 0))
    hyc[...] = row_scan(lyh + jnp.where(rows_i == 0, lyht[0:1], 0))
    jrow = iota((nj, nk), 0)
    klane = iota((nj, nk), 1)
    plane = ax[...]

    def field(i):
        return scan[i] + plane + by[pl.ds(i, 1), :]

    def stencil(i, low, mid, high):
        down_j = jnp.where(jrow == 0, by[pl.ds(i, 1), :], turn(mid, 1, 0))
        edge_j = jnp.where(last_y, 0, mid + hyc[pl.ds(i, 1), :])
        up_j = jnp.where(jrow == nj - 1, edge_j, turn(mid, nj - 1, 0))
        down_k = jnp.where(klane == 0, 0, turn(mid, 1, 1))
        edge_k = jnp.where(last_z, 0, mid)
        up_k = jnp.where(klane == nk - 1, edge_k, turn(mid, nk - 1, 1))
        v_ref[i] = 6 * mid + (low + high) + (down_j + up_j) + (down_k + up_k)

    def sweep(i, state):
        low, mid = state
        high = field(i + 1)
        stencil(i, low, mid, high)
        return mid, high

    low, mid = lax.fori_loop(0, ni - 1, sweep, (plane + lyt[0:1], field(0)))
    stencil(ni - 1, low, mid, jnp.where(last_x, 0, mid + hxc[...] + lyt[1:2]))

    up_sum("gz", z0, zup0, z0ss, z0rs, za0)
    up_sum("gz", z2, zup2, z2ss, z2rs, za2)
    down_wait("gz", d0, zdn0, 3)
    down_wait("gz", d2, zdn2, 4)
    up_sum("gz", z1, zup1, z1ss, z1rs, za1)
    down_wait("gz", d1, zdn1, 5)
    block = lax.rem(lanes, nb)

    def j_scan(w):
        for d in (1, 2, 4):
            w = w + jnp.where(subs >= d, pltpu.roll(w, d, 0), 0)
        whole = jnp.broadcast_to(w[SUB - 1 : SUB], w.shape)
        for d in range(1, nb):
            w = w + jnp.where(block >= d, turn(whole, d, 1), 0)
        return w

    def i_scan(w):
        d = nb
        while d < nl:
            w = w + jnp.where(lanes >= d, turn(w, d, 1), 0)
            d *= 2
        return w

    r2, r1 = za2[...], za1[...]
    y = i_scan(r1)
    y_low, y_high = y[0:1], y[1:2]
    corner, corner_high = r1[2:3], r1[3:4]
    D = i_scan(j_scan(za0[...] + jnp.where(lanes < nb, r2, 0))) + y_low
    xe = j_scan(r2)
    down_i = jnp.where(lanes < nb, xe + corner, turn(D, nb, 1))
    edge_i = jnp.where(last_x, 0, D + turn(xe, nl - 2 * nb, 1) + corner_high)
    up_i = jnp.where(lanes >= nl - nb, edge_i, turn(D, nl - nb, 1))
    t = pltpu.roll(D, 1, 0)
    down_j = jnp.where(subs == 0, jnp.where(block == 0, y_low, turn(t, 1, 1)), t)
    t = pltpu.roll(D, SUB - 1, 0)
    edge_j = jnp.where(last_y, 0, D + y_high)
    up_j = jnp.where(
        subs == SUB - 1, jnp.where(block == nb - 1, edge_j, turn(t, nl - 1, 1)), t
    )
    eh_ref[0:SUB] = 8 * D + (down_i + up_i) + (down_j + up_j)
    above = i_scan(j_scan(zdn0[...] + jnp.where(lanes < nb, zdn2[...], 0)))
    above = above + i_scan(zdn1[...])[0:1]
    eh_ref[SUB : 2 * SUB] = jnp.where(last_z, -D, above)

    for here, copy in ends:
        @pl.when(here)
        def _():
            copy().wait_send()


def finish(step_ref, v_ref, eh_ref, out_hbm, out, sems):
    ni, nj, nk = out.shape
    nb = nj // SUB
    scale = step_ref[0] * (1.0 / 12.0)
    at_end = iota((SUB, nk), 1) == nk - 1
    E, EH = eh_ref[0:SUB], eh_ref[0:SUB] + eh_ref[SUB : 2 * SUB]
    pieces = sems.shape[0]
    depth = ni // pieces
    copies = []
    for p in range(pieces):
        for i in range(p * depth, (p + 1) * depth):
            for b in range(nb):
                v = i * nb + b
                rows = slice(b * SUB, (b + 1) * SUB)
                carry = jnp.where(at_end, EH[:, v : v + 1], E[:, v : v + 1])
                out[i, rows, :] = (v_ref[i, rows, :] + carry).astype(F32) * scale
        part = pl.ds(p * depth, depth)
        copy = pltpu.make_async_copy(out.at[part], out_hbm.at[part], sems.at[p])
        copy.start()
        copies.append(copy)
    for copy in copies:
        copy.wait()


def solution(mesh):
    sizes = tuple(mesh.shape[a] for a in ("gx", "gy", "gz"))
    nx, ny, nz = sizes

    def on_device(quant_codes, error_step):
        ni, nj, nk = quant_codes.shape
        nl = ni * nj // SUB
        vm = lambda *shape: pltpu.VMEM(shape, I32)
        dma = lambda n: pltpu.SemaphoreType.DMA((n,))
        scratch = [
            vm(ni, nj, nk), vm(ni, nj, nk),
            vm(nj, nk), vm(nx - 1, nj, nk), vm(nj, nk),
            vm(ni, nk), vm(SUB, nk), vm(ny - 1, ni, nk), vm(ny - 1, SUB, nk),
            vm(ni, nk), vm(SUB, nk), vm(ni, nk), vm(SUB, nk),
            *[vm(SUB, nl)] * 3, *[vm(nz - 1, SUB, nl)] * 3,
            *[vm(SUB, nl)] * 6,
            vm(nj, nk), vm(nj, nk), vm(ni, nk), vm(SUB, nk),
            vm(nj, nk), vm(nj, nk), vm(ni, nk), vm(ni, nk),
            *[vm(SUB, nl)] * 3,
            pltpu.SemaphoreType.DMA,
            dma(nx - 1), dma(nx - 1), *[dma(ny - 1)] * 4, *[dma(nz - 1)] * 6,
            dma(6), dma(6),
        ]
        any_space = pl.BlockSpec(memory_space=pl.ANY)
        vmem = pl.BlockSpec(memory_space=pltpu.VMEM)
        v, eh = pl.pallas_call(
            functools.partial(exchange, sizes),
            out_shape=(
                jax.ShapeDtypeStruct((ni, nj, nk), I32),
                jax.ShapeDtypeStruct((2 * SUB, nl), I32),
            ),
            in_specs=[any_space],
            out_specs=(vmem, vmem),
            scratch_shapes=scratch,
            compiler_params=pltpu.CompilerParams(
                collective_id=0, has_side_effects=True, vmem_limit_bytes=16 * 2**20
            ),
            name="exchange",
        )(quant_codes)
        return pl.pallas_call(
            finish,
            out_shape=jax.ShapeDtypeStruct((ni, nj, nk), F32),
            in_specs=[pl.BlockSpec(memory_space=pltpu.SMEM), vmem, vmem],
            out_specs=any_space,
            scratch_shapes=[pltpu.VMEM((ni, nj, nk), F32), dma(4)],
            compiler_params=pltpu.CompilerParams(vmem_limit_bytes=16 * 2**20),
            name="finish",
        )(error_step, v, eh)

    return jax.shard_map(
        on_device, mesh=mesh, in_specs=(P("gx", "gy", "gz"), P()),
        out_specs=P("gx", "gy", "gz"), check_vma=False,
    )
```

time: 81.7 us -> 16 us (0.20)
  blocking collectives: 48.5 us -> 0 us
  starting transfers between devices: 16 us -> 0 us
  Pallas kernels: 0 us -> 14.1 us
  local copies, waits for them, and re-layouts: 9.16 us -> 1.03 us
  other arithmetic: 5.75 us -> 0 us
    all_gather x3 -> x0, blocking collectives: 48.5 us -> none  [prefix_2(): everything = lax.all_gather(value, axis)]
    ppermute x6 -> x0, starting transfers between devices: 16 us -> none  [passed_along(): return lax.ppermute(block, axis, route)]
    pallas_call x0 -> x2, Pallas kernels: none -> 14.1 us  [the longest x1 12.9 us: on_device(): pl.pallas_call(functools.partial(exchange, sizes), out_shape=(jax.ShapeDt...]
    slice x34 -> x0, local copies, waits for them, and re-layouts: 6.39 us -> none  [the longest x24 2.87 us: cumulate(): rolled = jnp.roll(values, offset, axis_dim)]
    add x20 -> x0, other arithmetic: 5.36 us -> none  [the longest x17 2.98 us: cumulate(): values + jnp.where(position >= offset, rolled, jnp.zeros_like(rolled))]
    add x1 -> x0, local copies, waits for them, and re-layouts: 1.1 us -> none  [on_device(): return recon + 0.5 * (neighbours / 6.0 - recon)]
  transfers between devices with their start and end apart: 6 -> 0, of which waited for: 1 -> 0; matrix products, arithmetic and copies ran while one was open for 4% -> 0% of each run, Pallas kernels for 0% -> 0%
where the time goes in v1:
time: 16 us; the launch traced here: 15.8 us
  Pallas kernels  14.1 us (88%)
  local copies, waits for them, and re-layouts  1.03 us (6%)
  between operations  0.67 us (4%)
    pallas_call x1, Pallas kernels, on_device(): pl.pallas_call(functools.partial(exchange, sizes), out_shape=(jax.ShapeDt...  12.9 us
    pallas_call x1, Pallas kernels, on_device(): pl.pallas_call(finish, out_shape=jax.ShapeDtypeStruct((ni, nj, nk), F32),...  1.19 us
    unnamed x2, local copies, waits for them, and re-layouts  1.03 us

profile of v1, /device:TPU:0, one launch (start us, length us, event | category | flops | bytes accessed | tf_op | source)
XLA Modules:
  0.0 15.8 jit_solution(10247841274000593455)
XLA Ops:
  0.7 0.0 copy-start
  0.7 1.0 %copy-done = s32[32,32,128]{2,1,0:T(8,128)S(1)} copy-done((s32[32,32,128]{2,1,0:T(8,128)S(1)}, s32[32,32,128]{2,1,0:T(8,128)}, u32[]{:S(2)}) %copy-start) | copy-done | bytes 524312
  1.7 12.9 %exchange.1 = (s32[32,32,128]{2,1,0:T(8,128)S(1)}, s32[16,128]{1,0:T(8,128)S(1)}) custom-call(s32[32,32,128]{2,1,0:T(8,128)S(1)} %copy-done), custom_call_target="tpu_custom_call" | custom-call | tf_op jit(solution)/shard_map/exchange/pallas_call | solution.py:369
  14.6 1.2 %finish.1 = f32[32,32,128]{2,1,0:T(8,128)} custom-call(f32[1]{0:T(128)S(6)} %copy.3.step_ref, s32[32,32,128]{2,1,0:T(8,128)S(1)} %get-tuple-element.7.v_ref, s32[16,128]{1,0:T(8,128)S(1)} %get-tuple-element.8.eh_ref), custom_call_target="tpu_custom_call" | custom-call | tf_op jit(solution)/shard_map/finish/pallas_call | solution.py:383
Async XLA Ops:
  0.7 1.0 %copy-start = (s32[32,32,128]{2,1,0:T(8,128)S(1)}, s32[32,32,128]{2,1,0:T(8,128)}, u32[]{:S(2)}) copy-start(s32[32,32,128]{2,1,0:T(8,128)} %q_hbm.1) | copy-start | bytes 1572868

commit v2 on v1

--- a/solution.py
+++ b/solution.py
@@ -11,6 +11,7 @@
 I32 = jnp.int32
 F32 = jnp.float32
 SUB = 8
+GRANT = 16 * 2**20
 
 
 def iota(shape, dim):
@@ -57,10 +58,10 @@
 
 def exchange(
     mesh_sizes, q_hbm, v_ref, eh_ref,
-    q, scan, xs, xup, xdn, ys, yt, yup, ytup, hy, ht, ydn, ytdn,
+    q, scan, xs, xup, xdn, ys, yup, hy, ydn, lines, cup, cx, cy,
     z0, z2, z1, zup0, zup2, zup1, d0, d2, d1, zdn0, zdn2, zdn1,
-    rx, hx, ry, ryt, ax, hxc, by, hyc, za0, za2, za1,
-    load_sem, xss, xrs, yss, yrs, ytss, ytrs, z0ss, z0rs, z2ss, z2rs, z1ss, z1rs, dss, drs,
+    rx, ry, ryt, ax, hxc, by, hyc, za0, za2, za1,
+    load_sem, xss, xrs, yss, yrs, css, crs, z0ss, z0rs, z2ss, z2rs, z1ss, z1rs, dss, drs, ready,
 ):
     nx, ny, nz = mesh_sizes
     ni, nj, nk = q.shape
@@ -74,17 +75,43 @@
     load = pltpu.make_async_copy(q_hbm, q, load_sem)
     load.start()
     barrier = pltpu.get_barrier_semaphore()
-    for axis in ("gz", "gy", "gx"):
+
+    def greet(to, axis, sem):
+        pl.semaphore_signal(sem, inc=1, device_id={axis: to}, device_id_type=MESH)
+
+    @pl.when(Z > 0)
+    def _():
+        greet(Z - 1, "gz", barrier)
+
+    @pl.when(Z < nz - 1)
+    def _():
+        greet(Z + 1, "gz", barrier)
+
+    for dx in range(nx):
+        for dy in range(ny):
+            if dx or dy:
+                pl.semaphore_signal(
+                    barrier, inc=1, device_id_type=MESH,
+                    device_id={"gx": lax.rem(X + dx, nx), "gy": lax.rem(Y + dy, ny)},
+                )
+
+    ends = []
+
+    def hear(d):
+        @pl.when(Z + d < nz)
+        def _():
+            pl.semaphore_wait(ready.at[d - 2], 1)
+
+            if d < nz - 1:
+                @pl.when(Z > 0)
+                def _():
+                    greet(Z - 1, "gz", ready.at[d - 1])
+
+    def up(axis, src, slots, ssem, rsem, first=False):
         for d in range(1, size[axis]):
-            pl.semaphore_signal(
-                barrier, inc=1, device_id={axis: lax.rem(place[axis] + d, size[axis])},
-                device_id_type=MESH,
-            )
-
-    ends = []
-
-    def up(axis, src, slots, ssem, rsem):
-        for d in range(1, size[axis]):
+            if first and d >= 2:
+                hear(d)
+
             def copy(d=d):
                 return pltpu.make_async_remote_copy(
                     src_ref=src, dst_ref=slots.at[d - 1], send_sem=ssem.at[d - 1],
@@ -144,15 +171,58 @@
     for i in range(1, ni):
         total = total + q[i]
     xs[...] = total
-    pl.semaphore_wait(barrier, nx + ny + nz - 3)
-    up("gx", xs, xup, xss, xrs)
-    down("gx", q.at[0], xdn, 0)
-
     for i in range(ni):
         ys[pl.ds(i, 1), :] = jnp.sum(q[i], axis=0, keepdims=True)
         hy[pl.ds(i, 1), :] = q[i, 0:1, :]
+    sk = iota((SUB, nk), 0)
+    lines[...] = jnp.where(
+        sk == 0, jnp.sum(total, axis=0, keepdims=True),
+        jnp.where(
+            sk == 1, jnp.sum(q[0], axis=0, keepdims=True),
+            jnp.where(sk == 2, total[0:1], 0),
+        ),
+    )
+    beside_z = (Z > 0).astype(I32) + (Z < nz - 1).astype(I32)
+    pl.semaphore_wait(barrier, nx * ny - 1 + beside_z)
+    up("gx", xs, xup, xss, xrs)
+    down("gx", q.at[0], xdn, 0)
     up("gy", ys, yup, yss, yrs)
     down("gy", hy, ydn, 1)
+
+    corners = []
+    for dx in range(-1, nx):
+        for dy in range(-1, ny):
+            if dx > 0 and dy > 0:
+                slot = cup.at[(dx - 1) * (ny - 1) + dy - 1]
+            elif dx == -1 and dy > 0:
+                slot = cx.at[dy - 1]
+            elif dx > 0 and dy == -1:
+                slot = cy.at[dx - 1]
+            else:
+                continue
+            corners.append((dx, dy, slot, len(corners)))
+
+    def inside(x, y):
+        return (x >= 0) & (x < nx) & (y >= 0) & (y < ny)
+
+    def corner_copy(dx, dy, slot, n):
+        return pltpu.make_async_remote_copy(
+            src_ref=lines, dst_ref=slot, send_sem=css.at[n], recv_sem=crs.at[n],
+            device_id={"gx": X + dx, "gy": Y + dy}, device_id_type=MESH,
+        )
+
+    for c in corners:
+        here = inside(X + c[0], Y + c[1])
+
+        @pl.when(here)
+        def _(c=c):
+            corner_copy(*c).start()
+
+        ends.append((here, functools.partial(corner_copy, *c)))
+    if nz > 2:
+        @pl.when((Z > 0) & (Z < nz - 1))
+        def _():
+            greet(Z - 1, "gz", ready.at[0])
 
     step = 8
 
@@ -163,18 +233,6 @@
         return 0
 
     lax.fori_loop(0, ni // step, scan_block, 0)
-
-    up_sum("gx", xs, xup, xss, xrs, rx)
-    down_wait("gx", q.at[0], xdn, 0)
-    rxv, hxv = rx[...], xdn[...]
-    sk = iota((SUB, nk), 0)
-    yt[...] = jnp.where(
-        sk == 0, jnp.sum(rxv, axis=0, keepdims=True),
-        jnp.where(sk == 1, jnp.sum(hxv, axis=0, keepdims=True), 0),
-    )
-    ht[...] = jnp.where(sk == 0, rxv[0:1], 0)
-    up("gy", yt, ytup, ytss, ytrs)
-    down("gy", ht, ytdn, 2)
 
     a0 = jnp.zeros((SUB, nl), I32)
     b0 = jnp.zeros((SUB, nl), I32)
@@ -186,8 +244,11 @@
             b0 = jnp.where(here, q[i, rows, 0:1], b0)
     z0[...] = a0
     d0[...] = b0
-    up("gz", z0, zup0, z0ss, z0rs)
-    down("gz", d0, zdn0, 3)
+    up("gz", z0, zup0, z0ss, z0rs, first=True)
+    down("gz", d0, zdn0, 2)
+    up_sum("gx", xs, xup, xss, xrs, rx)
+    down_wait("gx", q.at[0], xdn, 0)
+    rxv, hxv = rx[...], xdn[...]
     lx = lane_scan(jnp.concatenate([rxv, hxv], 0))
     a2 = jnp.zeros((SUB, nl), I32)
     b2 = jnp.zeros((SUB, nl), I32)
@@ -199,25 +260,25 @@
     z2[...] = a2
     d2[...] = b2
     up("gz", z2, zup2, z2ss, z2rs)
-    down("gz", d2, zdn2, 4)
+    down("gz", d2, zdn2, 3)
     ax[...] = row_scan(lx[:nj])
     hxc[...] = row_scan(lx[nj:])
 
-    def cumulate(i, before):
-        new = before + row_scan(scan[i])
-        scan[i] = new
-        return new
-
-    lax.fori_loop(0, ni, cumulate, jnp.zeros((nj, nk), I32))
-
     up_sum("gy", ys, yup, yss, yrs, ry)
-    up_sum("gy", yt, ytup, ytss, ytrs, ryt)
     down_wait("gy", hy, ydn, 1)
-    down_wait("gy", ht, ytdn, 2)
+    ryt[...] = jnp.zeros_like(ryt)
+    for c in corners:
+        row = 0 if c[0] > 0 and c[1] > 0 else 1 if c[1] > 0 else 2
+
+        @pl.when(inside(X - c[0], Y - c[1]))
+        def _(c=c, row=row):
+            corner_copy(*c).wait_recv()
+            ryt[...] += jnp.where(sk == row, c[2][...], 0)
+
     ryv, rytv = ry[...], ryt[...]
-    ly = lane_scan(jnp.concatenate([ryv, ydn[...], rytv, ytdn[...]], 0))
-    lyl, lyh = ly[:ni], ly[ni : 2 * ni]
-    lyt, lyht = ly[2 * ni : 2 * ni + SUB], ly[2 * ni + SUB :]
+    ly = lane_scan(jnp.concatenate([ryv, ydn[...], rytv], 0))
+    lyl, lyh, lyt = ly[:ni], ly[ni : 2 * ni], ly[2 * ni :]
+    lyht = lyt[2:3]
     mine = (iota((ni, nl), 1) // nb) == iota((ni, nl), 0)
     first = (iota((1, nl), 1) // nb) == 0
 
@@ -237,7 +298,7 @@
     )
     d1[...] = jnp.where(subs == 0, along(ryv[:, 0:1], rytv[0:1, 0:1]), 0)
     up("gz", z1, zup1, z1ss, z1rs)
-    down("gz", d1, zdn1, 5)
+    down("gz", d1, zdn1, 4)
 
     rows_i = iota((ni, nk), 0)
     by[...] = row_scan(lyl + jnp.where(rows_i == 0, lyt[0:1], 0))
@@ -246,8 +307,9 @@
     klane = iota((nj, nk), 1)
     plane = ax[...]
 
-    def field(i):
-        return scan[i] + plane + by[pl.ds(i, 1), :]
+    def field(i, before):
+        inner = before + row_scan(scan[i])
+        return inner, inner + plane + by[pl.ds(i, 1), :]
 
     def stencil(i, low, mid, high):
         down_j = jnp.where(jrow == 0, by[pl.ds(i, 1), :], turn(mid, 1, 0))
@@ -259,20 +321,21 @@
         v_ref[i] = 6 * mid + (low + high) + (down_j + up_j) + (down_k + up_k)
 
     def sweep(i, state):
-        low, mid = state
-        high = field(i + 1)
+        low, mid, before = state
+        inner, high = field(i + 1, before)
         stencil(i, low, mid, high)
-        return mid, high
-
-    low, mid = lax.fori_loop(0, ni - 1, sweep, (plane + lyt[0:1], field(0)))
+        return mid, high, inner
+
+    inner, mid = field(0, jnp.zeros((nj, nk), I32))
+    low, mid, _ = lax.fori_loop(0, ni - 1, sweep, (plane + lyt[0:1], mid, inner))
     stencil(ni - 1, low, mid, jnp.where(last_x, 0, mid + hxc[...] + lyt[1:2]))
 
     up_sum("gz", z0, zup0, z0ss, z0rs, za0)
     up_sum("gz", z2, zup2, z2ss, z2rs, za2)
-    down_wait("gz", d0, zdn0, 3)
-    down_wait("gz", d2, zdn2, 4)
+    down_wait("gz", d0, zdn0, 2)
+    down_wait("gz", d2, zdn2, 3)
     up_sum("gz", z1, zup1, z1ss, z1rs, za1)
-    down_wait("gz", d1, zdn1, 5)
+    down_wait("gz", d1, zdn1, 4)
     block = lax.rem(lanes, nb)
 
     def j_scan(w):
@@ -353,18 +416,22 @@
         scratch = [
             vm(ni, nj, nk), vm(ni, nj, nk),
             vm(nj, nk), vm(nx - 1, nj, nk), vm(nj, nk),
-            vm(ni, nk), vm(SUB, nk), vm(ny - 1, ni, nk), vm(ny - 1, SUB, nk),
-            vm(ni, nk), vm(SUB, nk), vm(ni, nk), vm(SUB, nk),
+            vm(ni, nk), vm(ny - 1, ni, nk), vm(ni, nk), vm(ni, nk),
+            vm(SUB, nk), vm((nx - 1) * (ny - 1), SUB, nk),
+            vm(ny - 1, SUB, nk), vm(nx - 1, SUB, nk),
             *[vm(SUB, nl)] * 3, *[vm(nz - 1, SUB, nl)] * 3,
             *[vm(SUB, nl)] * 6,
-            vm(nj, nk), vm(nj, nk), vm(ni, nk), vm(SUB, nk),
+            vm(nj, nk), vm(ni, nk), vm(SUB, nk),
             vm(nj, nk), vm(nj, nk), vm(ni, nk), vm(ni, nk),
             *[vm(SUB, nl)] * 3,
             pltpu.SemaphoreType.DMA,
-            dma(nx - 1), dma(nx - 1), *[dma(ny - 1)] * 4, *[dma(nz - 1)] * 6,
-            dma(6), dma(6),
+            dma(nx - 1), dma(nx - 1), dma(ny - 1), dma(ny - 1),
+            dma(nx * ny - 1 + nx * ny), dma(nx * ny - 1 + nx * ny), *[dma(nz - 1)] * 6,
+            dma(5), dma(5),
+            pltpu.SemaphoreType.REGULAR((max(nz - 2, 1),)),
         ]
         any_space = pl.BlockSpec(memory_space=pl.ANY)
+        hbm = pl.BlockSpec(memory_space=pltpu.HBM)
         vmem = pl.BlockSpec(memory_space=pltpu.VMEM)
         v, eh = pl.pallas_call(
             functools.partial(exchange, sizes),
@@ -372,14 +439,14 @@
                 jax.ShapeDtypeStruct((ni, nj, nk), I32),
                 jax.ShapeDtypeStruct((2 * SUB, nl), I32),
             ),
-            in_specs=[any_space],
+            in_specs=[hbm],
             out_specs=(vmem, vmem),
             scratch_shapes=scratch,
             compiler_params=pltpu.CompilerParams(
-                collective_id=0, has_side_effects=True, vmem_limit_bytes=16 * 2**20
+                collective_id=0, has_side_effects=True, vmem_limit_bytes=GRANT
             ),
             name="exchange",
-        )(quant_codes)
+        )(pltpu.with_memory_space_constraint(quant_codes, pltpu.HBM))
         return pl.pallas_call(
             finish,
             out_shape=jax.ShapeDtypeStruct((ni, nj, nk), F32),

time: 16 us -> 13.4 us (0.84)
  Pallas kernels: 14.1 us -> 12.6 us
  local copies, waits for them, and re-layouts: 1.03 us -> 0 us
    pallas_call x1, Pallas kernels: 12.9 us -> 11.4 us  [on_device(): pl.pallas_call(functools.partial(exchange, sizes), out_shape=(jax.ShapeDt...]
    unnamed x2 -> x0, local copies, waits for them, and re-layouts: 1.03 us -> none
where the time goes in v2:
time: 13.4 us; the launch traced here: 13.3 us
  Pallas kernels  12.6 us (94%)
  between operations  0.66 us (5%)
    pallas_call x1, Pallas kernels, on_device(): pl.pallas_call(functools.partial(exchange, sizes), out_shape=(jax.ShapeDt...  11.4 us
    pallas_call x1, Pallas kernels, on_device(): pl.pallas_call(finish, out_shape=jax.ShapeDtypeStruct((ni, nj, nk), F32),...  1.19 us

profile of v2, /device:TPU:0, one launch (start us, length us, event | category | flops | bytes accessed | tf_op | source)
XLA Modules:
  0.0 13.3 jit_solution(965107574057136850)
XLA Ops:
  0.7 11.4 %exchange.1 = (s32[32,32,128]{2,1,0:T(8,128)S(1)}, s32[16,128]{1,0:T(8,128)S(1)}) custom-call(s32[32,32,128]{2,1,0:T(8,128)} %q_hbm.1), custom_call_target="tpu_custom_call" | custom-call | tf_op jit(solution)/shard_map/exchange/pallas_call | solution.py:436
  12.1 1.2 %finish.1 = f32[32,32,128]{2,1,0:T(8,128)} custom-call(f32[1]{0:T(128)S(6)} %copy.3.step_ref, s32[32,32,128]{2,1,0:T(8,128)S(1)} %get-tuple-element.7.v_ref, s32[16,128]{1,0:T(8,128)S(1)} %get-tuple-element.8.eh_ref), custom_call_target="tpu_custom_call" | custom-call | tf_op jit(solution)/shard_map/finish/pallas_call | solution.py:450

commit v3 on v2

--- a/solution.py
+++ b/solution.py
@@ -12,6 +12,7 @@
 F32 = jnp.float32
 SUB = 8
 GRANT = 16 * 2**20
+UNROLL = 4
 
 
 def iota(shape, dim):
@@ -59,9 +60,8 @@
 def exchange(
     mesh_sizes, q_hbm, v_ref, eh_ref,
     q, scan, xs, xup, xdn, ys, yup, hy, ydn, lines, cup, cx, cy,
-    z0, z2, z1, zup0, zup2, zup1, d0, d2, d1, zdn0, zdn2, zdn1,
-    rx, ry, ryt, ax, hxc, by, hyc, za0, za2, za1,
-    load_sem, xss, xrs, yss, yrs, css, crs, z0ss, z0rs, z2ss, z2rs, z1ss, z1rs, dss, drs, ready,
+    zs, zup, ds, zdn, rx, ry, ryt, ax, hxc, by, hyc, carry,
+    load_sem, xss, xrs, yss, yrs, css, crs, zss, zrs, dss, drs, ready,
 ):
     nx, ny, nz = mesh_sizes
     ni, nj, nk = q.shape
@@ -107,11 +107,8 @@
                 def _():
                     greet(Z - 1, "gz", ready.at[d - 1])
 
-    def up(axis, src, slots, ssem, rsem, first=False):
-        for d in range(1, size[axis]):
-            if first and d >= 2:
-                hear(d)
-
+    def up(axis, src, slots, ssem, rsem, steps=None):
+        for d in steps or range(1, size[axis]):
             def copy(d=d):
                 return pltpu.make_async_remote_copy(
                     src_ref=src, dst_ref=slots.at[d - 1], send_sem=ssem.at[d - 1],
@@ -184,10 +181,8 @@
     )
     beside_z = (Z > 0).astype(I32) + (Z < nz - 1).astype(I32)
     pl.semaphore_wait(barrier, nx * ny - 1 + beside_z)
-    up("gx", xs, xup, xss, xrs)
-    down("gx", q.at[0], xdn, 0)
+    down("gy", hy, ydn, 1)
     up("gy", ys, yup, yss, yrs)
-    down("gy", hy, ydn, 1)
 
     corners = []
     for dx in range(-1, nx):
@@ -219,6 +214,8 @@
             corner_copy(*c).start()
 
         ends.append((here, functools.partial(corner_copy, *c)))
+    up("gx", xs, xup, xss, xrs)
+    down("gx", q.at[0], xdn, 0)
     if nz > 2:
         @pl.when((Z > 0) & (Z < nz - 1))
         def _():
@@ -233,6 +230,23 @@
         return 0
 
     lax.fori_loop(0, ni // step, scan_block, 0)
+
+    block = lax.rem(lanes, nb)
+
+    def j_scan(w):
+        for d in (1, 2, 4):
+            w = w + jnp.where(subs >= d, pltpu.roll(w, d, 0), 0)
+        whole = jnp.broadcast_to(w[SUB - 1 : SUB], w.shape)
+        for d in range(1, nb):
+            w = w + jnp.where(block >= d, turn(whole, d, 1), 0)
+        return w
+
+    def i_scan(w):
+        d = nb
+        while d < nl:
+            w = w + jnp.where(lanes >= d, turn(w, d, 1), 0)
+            d *= 2
+        return w
 
     a0 = jnp.zeros((SUB, nl), I32)
     b0 = jnp.zeros((SUB, nl), I32)
@@ -242,10 +256,6 @@
             here = lanes == i * nb + b
             a0 = jnp.where(here, scan[i, rows, nk - 1 : nk], a0)
             b0 = jnp.where(here, q[i, rows, 0:1], b0)
-    z0[...] = a0
-    d0[...] = b0
-    up("gz", z0, zup0, z0ss, z0rs, first=True)
-    down("gz", d0, zdn0, 2)
     up_sum("gx", xs, xup, xss, xrs, rx)
     down_wait("gx", q.at[0], xdn, 0)
     rxv, hxv = rx[...], xdn[...]
@@ -257,10 +267,14 @@
         a2 = jnp.where(lanes == b, lx[rows, nk - 1 : nk], a2)
         if b < nb:
             b2 = jnp.where(lanes == b, rxv[rows, 0:1], b2)
-    z2[...] = a2
-    d2[...] = b2
-    up("gz", z2, zup2, z2ss, z2rs)
-    down("gz", d2, zdn2, 3)
+    a0 = i_scan(j_scan(a0 + jnp.where(lanes < nb, a2, 0)))
+    b0 = i_scan(j_scan(b0 + jnp.where(lanes < nb, b2, 0)))
+    a2 = j_scan(a2)
+    for d in range(2, nz):
+        @pl.when(Z > 0)
+        def _(d=d):
+            hear(d)
+
     ax[...] = row_scan(lx[:nj])
     hxc[...] = row_scan(lx[nj:])
 
@@ -279,26 +293,20 @@
     ly = lane_scan(jnp.concatenate([ryv, ydn[...], rytv], 0))
     lyl, lyh, lyt = ly[:ni], ly[ni : 2 * ni], ly[2 * ni :]
     lyht = lyt[2:3]
-    mine = (iota((ni, nl), 1) // nb) == iota((ni, nl), 0)
-    first = (iota((1, nl), 1) // nb) == 0
+    upto = (iota((ni, nl), 1) // nb) >= iota((ni, nl), 0)
 
     def along(column, extra):
-        row = jnp.sum(jnp.where(mine, column, 0), axis=0, keepdims=True)
-        return row + jnp.where(first, extra, 0)
+        return jnp.sum(jnp.where(upto, column, 0), axis=0, keepdims=True) + extra
 
     end = slice(nk - 1, nk)
-    z1[...] = jnp.where(
-        subs == 0, along(lyl[:, end], lyt[0:1, end]),
-        jnp.where(
-            subs == 1, along(lyh[:, end], lyht[0:1, end]),
-            jnp.where(
-                subs == 2, lyt[0:1, end], jnp.where(subs == 3, lyt[1:2, end], 0)
-            ),
-        ),
-    )
-    d1[...] = jnp.where(subs == 0, along(ryv[:, 0:1], rytv[0:1, 0:1]), 0)
-    up("gz", z1, zup1, z1ss, z1rs)
-    down("gz", d1, zdn1, 4)
+    y_low = along(lyl[:, end], lyt[0:1, end])
+    y_high = along(lyh[:, end], lyht[0:1, end])
+    zs[0:SUB] = a0 + y_low
+    zs[SUB : 2 * SUB] = a2 + jnp.where(lanes < nb, lyt[0:1, end], lyt[1:2, end])
+    zs[2 * SUB :] = jnp.where(subs == 0, y_low, jnp.where(subs == 1, y_high, 0))
+    ds[...] = b0 + along(ryv[:, 0:1], rytv[0:1, 0:1])
+    down("gz", ds, zdn, 2)
+    up("gz", zs, zup, zss, zrs, [1])
 
     rows_i = iota((ni, nk), 0)
     by[...] = row_scan(lyl + jnp.where(rows_i == 0, lyt[0:1], 0))
@@ -327,40 +335,33 @@
         return mid, high, inner
 
     inner, mid = field(0, jnp.zeros((nj, nk), I32))
-    low, mid, _ = lax.fori_loop(0, ni - 1, sweep, (plane + lyt[0:1], mid, inner))
+    state = (plane + lyt[0:1], mid, inner)
+    many = (ni - 1) // UNROLL
+
+    def sweeps(g, state):
+        for u in range(UNROLL):
+            state = sweep(g * UNROLL + u, state)
+        return state
+
+    state = lax.fori_loop(0, many, sweeps, state)
+    for i in range(many * UNROLL, ni - 1):
+        state = sweep(i, state)
+    low, mid, _ = state
     stencil(ni - 1, low, mid, jnp.where(last_x, 0, mid + hxc[...] + lyt[1:2]))
 
-    up_sum("gz", z0, zup0, z0ss, z0rs, za0)
-    up_sum("gz", z2, zup2, z2ss, z2rs, za2)
-    down_wait("gz", d0, zdn0, 2)
-    down_wait("gz", d2, zdn2, 3)
-    up_sum("gz", z1, zup1, z1ss, z1rs, za1)
-    down_wait("gz", d1, zdn1, 4)
-    block = lax.rem(lanes, nb)
-
-    def j_scan(w):
-        for d in (1, 2, 4):
-            w = w + jnp.where(subs >= d, pltpu.roll(w, d, 0), 0)
-        whole = jnp.broadcast_to(w[SUB - 1 : SUB], w.shape)
-        for d in range(1, nb):
-            w = w + jnp.where(block >= d, turn(whole, d, 1), 0)
-        return w
-
-    def i_scan(w):
-        d = nb
-        while d < nl:
-            w = w + jnp.where(lanes >= d, turn(w, d, 1), 0)
-            d *= 2
-        return w
-
-    r2, r1 = za2[...], za1[...]
-    y = i_scan(r1)
-    y_low, y_high = y[0:1], y[1:2]
-    corner, corner_high = r1[2:3], r1[3:4]
-    D = i_scan(j_scan(za0[...] + jnp.where(lanes < nb, r2, 0))) + y_low
-    xe = j_scan(r2)
-    down_i = jnp.where(lanes < nb, xe + corner, turn(D, nb, 1))
-    edge_i = jnp.where(last_x, 0, D + turn(xe, nl - 2 * nb, 1) + corner_high)
+    for d in range(2, nz):
+        @pl.when(Z == 0)
+        def _(d=d):
+            hear(d)
+
+        up("gz", zs, zup, zss, zrs, [d])
+
+    up_sum("gz", zs, zup, zss, zrs, carry)
+    down_wait("gz", ds, zdn, 2)
+    D, xe = carry[0:SUB], carry[SUB : 2 * SUB]
+    y_low, y_high = carry[2 * SUB : 2 * SUB + 1], carry[2 * SUB + 1 : 2 * SUB + 2]
+    down_i = jnp.where(lanes < nb, xe, turn(D, nb, 1))
+    edge_i = jnp.where(last_x, 0, D + turn(xe, nl - 2 * nb, 1))
     up_i = jnp.where(lanes >= nl - nb, edge_i, turn(D, nl - nb, 1))
     t = pltpu.roll(D, 1, 0)
     down_j = jnp.where(subs == 0, jnp.where(block == 0, y_low, turn(t, 1, 1)), t)
@@ -370,9 +371,7 @@
         subs == SUB - 1, jnp.where(block == nb - 1, edge_j, turn(t, nl - 1, 1)), t
     )
     eh_ref[0:SUB] = 8 * D + (down_i + up_i) + (down_j + up_j)
-    above = i_scan(j_scan(zdn0[...] + jnp.where(lanes < nb, zdn2[...], 0)))
-    above = above + i_scan(zdn1[...])[0:1]
-    eh_ref[SUB : 2 * SUB] = jnp.where(last_z, -D, above)
+    eh_ref[SUB : 2 * SUB] = jnp.where(last_z, -D, zdn[...])
 
     for here, copy in ends:
         @pl.when(here)
@@ -419,15 +418,14 @@
             vm(ni, nk), vm(ny - 1, ni, nk), vm(ni, nk), vm(ni, nk),
             vm(SUB, nk), vm((nx - 1) * (ny - 1), SUB, nk),
             vm(ny - 1, SUB, nk), vm(nx - 1, SUB, nk),
-            *[vm(SUB, nl)] * 3, *[vm(nz - 1, SUB, nl)] * 3,
-            *[vm(SUB, nl)] * 6,
+            vm(3 * SUB, nl), vm(nz - 1, 3 * SUB, nl), vm(SUB, nl), vm(SUB, nl),
             vm(nj, nk), vm(ni, nk), vm(SUB, nk),
             vm(nj, nk), vm(nj, nk), vm(ni, nk), vm(ni, nk),
-            *[vm(SUB, nl)] * 3,
+            vm(3 * SUB, nl),
             pltpu.SemaphoreType.DMA,
             dma(nx - 1), dma(nx - 1), dma(ny - 1), dma(ny - 1),
-            dma(nx * ny - 1 + nx * ny), dma(nx * ny - 1 + nx * ny), *[dma(nz - 1)] * 6,
-            dma(5), dma(5),
+            dma(nx * ny - 1 + nx * ny), dma(nx * ny - 1 + nx * ny), dma(nz - 1), dma(nz - 1),
+            dma(3), dma(3),
             pltpu.SemaphoreType.REGULAR((max(nz - 2, 1),)),
         ]
         any_space = pl.BlockSpec(memory_space=pl.ANY)

time: 13.4 us -> 12.3 us (0.918)
  Pallas kernels: 12.6 us -> 11.5 us
    pallas_call x1, Pallas kernels: 11.4 us -> 10.3 us  [on_device(): pl.pallas_call(functools.partial(exchange, sizes), out_shape=(jax.ShapeDt...]
where the time goes in v3:
time: 12.3 us; the launch traced here: 12.2 us
  Pallas kernels  11.5 us (93%)
  between operations  0.66 us (5%)
    pallas_call x1, Pallas kernels, on_device(): pl.pallas_call(functools.partial(exchange, sizes), out_shape=(jax.ShapeDt...  10.3 us
    pallas_call x1, Pallas kernels, on_device(): pl.pallas_call(finish, out_shape=jax.ShapeDtypeStruct((ni, nj, nk), F32),...  1.19 us

profile of v3, /device:TPU:0, one launch (start us, length us, event | category | flops | bytes accessed | tf_op | source)
XLA Modules:
  0.0 12.2 jit_solution(10048708235459073319)
XLA Ops:
  0.7 10.3 %exchange.1 = (s32[32,32,128]{2,1,0:T(8,128)S(1)}, s32[16,128]{1,0:T(8,128)S(1)}) custom-call(s32[32,32,128]{2,1,0:T(8,128)} %q_hbm.1), custom_call_target="tpu_custom_call" | custom-call | tf_op jit(solution)/shard_map/exchange/pallas_call | solution.py:434
  11.0 1.2 %finish.1 = f32[32,32,128]{2,1,0:T(8,128)} custom-call(f32[1]{0:T(128)S(6)} %copy.3.step_ref, s32[32,32,128]{2,1,0:T(8,128)S(1)} %get-tuple-element.7.v_ref, s32[16,128]{1,0:T(8,128)S(1)} %get-tuple-element.8.eh_ref), custom_call_target="tpu_custom_call" | custom-call | tf_op jit(solution)/shard_map/finish/pallas_call | solution.py:448

commit v4 on v3

--- a/solution.py
+++ b/solution.py
@@ -279,33 +279,39 @@
     hxc[...] = row_scan(lx[nj:])
 
     up_sum("gy", ys, yup, yss, yrs, ry)
+    ryt[...] = jnp.zeros_like(ryt)
+
+    def gather_lines(wanted):
+        for c in corners:
+            row = 0 if c[0] > 0 and c[1] > 0 else 1 if c[1] > 0 else 2
+            if (row == 0) != wanted:
+                continue
+
+            @pl.when(inside(X - c[0], Y - c[1]))
+            def _(c=c, row=row):
+                corner_copy(*c).wait_recv()
+                ryt[...] += jnp.where(sk == row, c[2][...], 0)
+
+    upto = (iota((ni, nl), 1) // nb) >= iota((ni, nl), 0)
+
+    def along(column, extra):
+        return jnp.sum(jnp.where(upto, column, 0), axis=0, keepdims=True) + extra
+
+    gather_lines(True)
+    ds[...] = b0 + along(ry[:, 0:1], ryt[0:1, 0:1])
+    down("gz", ds, zdn, 2)
     down_wait("gy", hy, ydn, 1)
-    ryt[...] = jnp.zeros_like(ryt)
-    for c in corners:
-        row = 0 if c[0] > 0 and c[1] > 0 else 1 if c[1] > 0 else 2
-
-        @pl.when(inside(X - c[0], Y - c[1]))
-        def _(c=c, row=row):
-            corner_copy(*c).wait_recv()
-            ryt[...] += jnp.where(sk == row, c[2][...], 0)
-
+    gather_lines(False)
     ryv, rytv = ry[...], ryt[...]
     ly = lane_scan(jnp.concatenate([ryv, ydn[...], rytv], 0))
     lyl, lyh, lyt = ly[:ni], ly[ni : 2 * ni], ly[2 * ni :]
     lyht = lyt[2:3]
-    upto = (iota((ni, nl), 1) // nb) >= iota((ni, nl), 0)
-
-    def along(column, extra):
-        return jnp.sum(jnp.where(upto, column, 0), axis=0, keepdims=True) + extra
-
     end = slice(nk - 1, nk)
     y_low = along(lyl[:, end], lyt[0:1, end])
     y_high = along(lyh[:, end], lyht[0:1, end])
     zs[0:SUB] = a0 + y_low
     zs[SUB : 2 * SUB] = a2 + jnp.where(lanes < nb, lyt[0:1, end], lyt[1:2, end])
     zs[2 * SUB :] = jnp.where(subs == 0, y_low, jnp.where(subs == 1, y_high, 0))
-    ds[...] = b0 + along(ryv[:, 0:1], rytv[0:1, 0:1])
-    down("gz", ds, zdn, 2)
     up("gz", zs, zup, zss, zrs, [1])
 
     rows_i = iota((ni, nk), 0)

time: 12.3 us -> 11.8 us (0.959)
  Pallas kernels: 11.5 us -> 10.9 us
    pallas_call x1, Pallas kernels: 10.3 us -> 9.76 us  [on_device(): pl.pallas_call(functools.partial(exchange, sizes), out_shape=(jax.ShapeDt...]
where the time goes in v4:
time: 11.8 us; the launch traced here: 11.6 us
  Pallas kernels  10.9 us (92%)
  between operations  0.66 us (6%)
    pallas_call x1, Pallas kernels, on_device(): pl.pallas_call(functools.partial(exchange, sizes), out_shape=(jax.ShapeDt...  9.76 us
    pallas_call x1, Pallas kernels, on_device(): pl.pallas_call(finish, out_shape=jax.ShapeDtypeStruct((ni, nj, nk), F32),...  1.19 us

profile of v4, /device:TPU:0, one launch (start us, length us, event | category | flops | bytes accessed | tf_op | source)
XLA Modules:
  0.0 11.6 jit_solution(17103797599845037884)
XLA Ops:
  0.7 9.8 %exchange.1 = (s32[32,32,128]{2,1,0:T(8,128)S(1)}, s32[16,128]{1,0:T(8,128)S(1)}) custom-call(s32[32,32,128]{2,1,0:T(8,128)} %q_hbm.1), custom_call_target="tpu_custom_call" | custom-call | tf_op jit(solution)/shard_map/exchange/pallas_call | solution.py:440
  10.4 1.2 %finish.1 = f32[32,32,128]{2,1,0:T(8,128)} custom-call(f32[1]{0:T(128)S(6)} %copy.3.step_ref, s32[32,32,128]{2,1,0:T(8,128)S(1)} %get-tuple-element.7.v_ref, s32[16,128]{1,0:T(8,128)S(1)} %get-tuple-element.8.eh_ref), custom_call_target="tpu_custom_call" | custom-call | tf_op jit(solution)/shard_map/finish/pallas_call | solution.py:454
